TPU v7x, 256 devices: a whole 4x4x8 slice. The times are simulated.
256 devices in a mesh: grp: 32 (over z_hi, y, core), tp: 8 (over z_lo, x).
Axes of the slice: x: 4, y: 4, z: 8 (z_hi: 4, z_lo: 2; z = z_hi * 2 + z_lo), core: 2. Of those that a mesh axis runs over, the one named last changes fastest.
Arguments:
- tokens: bfloat16 [2048, 6144], P('grp', 'tp'), may hold values from -6 to 6
- norm_gain: float32 [6144], replicated, may hold values from 0.25 to 1.75
- router_weight: bfloat16 [6144, 8], replicated, may hold values from -0.078125 to 0.078125
- expert_ids: int32 [2048, 2], P('grp'), may hold values from 0 to 7, all different within a row; in each aligned block of 64 rows (0 to 63, 64 to 127, ...) at most 18 rows name the same one
- gate_proj: bfloat16 [6144, 65536], P(None, ('grp', 'tp')), may hold values from -0.078125 to 0.078125
- up_proj: bfloat16 [6144, 65536], P(None, ('grp', 'tp')), may hold values from -0.078125 to 0.078125
- down_proj: bfloat16 [65536, 6144], P(('grp', 'tp')), may hold values from -0.25 to 0.25
Outputs:
- mixed: bfloat16 [2048, 6144], P('grp', 'tp')
Inputs may be any that keep to these rules, and one draw needn't show every extreme that they name: `expert_ids`: each row names two different experts; within the rows of one group (aligned blocks of 64 rows) no expert is named more than 18 times, and in some group one expert is named exactly 18 times.
All inputs are finite; a program needn't handle non-finite values.
Results may differ from a plain program's by a relative error of at most 0.017.
Values may be sent and summed in bfloat16 or wider, within the bound.
A program may use at most 128 MiB of HBM per device.

v0:
```python
from functools import partial

import jax
import jax.numpy as jnp
from jax import lax
from jax.sharding import Mesh
from jax.sharding import PartitionSpec as P

CAP = 18
GRP = ("grp_0", "grp_1", "grp_2")
GRP_TP = ("grp_0", "grp_1", "grp_2", "tp")


epsilon = 1e-05


def copy_for_each(x, axis):
    copies = jnp.broadcast_to(x, (lax.axis_size(axis), *x.shape))
    return lax.all_to_all(copies, axis, split_axis=0, concat_axis=0, tiled=True)


def taken_together(x, axis):
    return copy_for_each(x, axis).sum(axis=0)


def in_blocks(x, dim, size):
    lengths = x.shape
    blocks = x.reshape(*lengths[:dim], size, lengths[dim] // size, *lengths[dim + 1 :])
    return jnp.moveaxis(blocks, dim, 0)


def joined_along(blocks, dim):
    blocks = jnp.moveaxis(blocks, 0, dim)
    lengths = blocks.shape
    return blocks.reshape(*lengths[:dim], lengths[dim] * lengths[dim + 1], *lengths[dim + 2 :])


def exchange_in_order(blocks, axes, order):
    inside = blocks.shape[1:]
    out = blocks.reshape(*(lax.axis_size(a) for a in axes), *inside)
    for k in order:
        out = lax.all_to_all(out, axes[k], k, k, tiled=True)
    return out.reshape(-1, *inside)


def two_step_exchange(x, groups, order, split_dim, concat_dim):
    size = lax.axis_size(groups[0]) * lax.axis_size(groups[1])
    blocks = in_blocks(x, split_dim, size)
    return joined_along(exchange_in_order(blocks, groups, order), concat_dim)


def expert_rows(gate_proj, up_proj, down_proj, gather_first, received):
    received = lax.all_gather(received, "tp", axis=2, tiled=True)
    source_groups, slot_count, feature_width = received.shape
    row_block = received.reshape(source_groups * slot_count, feature_width)
    gate_act = jnp.dot(row_block, gate_proj, preferred_element_type=jnp.float32)
    up_act = jnp.dot(row_block, up_proj, preferred_element_type=jnp.float32)
    hidden = (jax.nn.silu(gate_act) * up_act).astype(jnp.bfloat16)
    partial_out = jnp.dot(hidden, down_proj, preferred_element_type=jnp.float32).astype(
        jnp.bfloat16
    )
    partial_out = partial_out.reshape(source_groups, slot_count, feature_width)
    own_share = (
        lax.psum_scatter(partial_out, "tp", scatter_dimension=2, tiled=True)
        .astype(jnp.float32)
        .astype(jnp.bfloat16)
    )
    return lax.all_to_all(own_share, GRP, split_axis=0, concat_axis=0, tiled=True)


def per_device(tokens, norm_gain, router_weight, expert_ids, gate_proj, up_proj, down_proj):
    tok_rows, local_width = tokens.shape
    experts = router_weight.shape[1]
    groups = lax.axis_size(GRP)
    owners = groups // experts
    capacity = CAP
    local_rows = tokens.astype(jnp.float32)
    width_all = local_width * lax.axis_size("tp")
    offset_start = lax.axis_index("tp") * local_width
    gain_part = lax.dynamic_slice_in_dim(norm_gain, offset_start, local_width, 0)
    router_part = lax.dynamic_slice_in_dim(router_weight, offset_start, local_width, 0)
    squares = taken_together(jnp.sum(local_rows * local_rows, axis=-1, keepdims=True), "tp")
    normed = (local_rows * lax.rsqrt(squares / width_all + epsilon) * gain_part).astype(
        jnp.bfloat16
    )
    logits = taken_together(jnp.dot(normed, router_part, preferred_element_type=jnp.float32), "tp")
    expert_iota = jnp.arange(experts, dtype=jnp.int32)[None, :]
    chosen_first = (expert_ids[:, 0:1] == expert_iota).astype(jnp.int32)
    chosen_second = (expert_ids[:, 1:2] == expert_iota).astype(jnp.int32)
    first_logit = jnp.sum(logits * chosen_first.astype(jnp.float32), axis=-1)
    second = jnp.sum(logits * chosen_second.astype(jnp.float32), axis=-1)
    gate_first = 1.0 / (1.0 + jnp.exp(second - first_logit))
    gate_second = 1.0 / (1.0 + jnp.exp(first_logit - second))
    gate_table = gate_first[:, None] * chosen_first.astype(jnp.float32) + gate_second[
        :, None
    ] * chosen_second.astype(jnp.float32)
    routed = chosen_first + chosen_second
    slot_index = jnp.cumsum(routed, axis=0) - 1
    slot_iota = jnp.arange(capacity, dtype=jnp.int32)
    slot_picks = (slot_index.T[:, None, :] == slot_iota[None, :, None]) & (
        routed.T[:, None, :] == 1
    )
    selector = slot_picks.astype(jnp.bfloat16)
    per_expert = jnp.einsum(
        "ect,td->ecd", selector, normed, preferred_element_type=jnp.float32
    ).astype(jnp.bfloat16)
    outgoing = jnp.repeat(per_expert, owners, axis=0)
    worker = partial(expert_rows, gate_proj, up_proj, down_proj, True)
    returned = worker(two_step_exchange(outgoing, (("grp_0", "grp_1"), "grp_2"), (1, 0), 0, 0))
    summed = (
        returned.astype(jnp.float32).reshape(experts, owners, capacity, local_width).sum(axis=1)
    )
    combine = slot_picks.astype(jnp.float32) * gate_table.T[:, None, :]
    mixed = jnp.einsum("ect,ecd->td", combine, summed)
    return mixed.astype(jnp.bfloat16)


def solution(mesh):
    split = Mesh(mesh.devices.reshape(4, 4, 2, mesh.shape["tp"]), ("grp_0", "grp_1", "grp_2", "tp"))
    placed = (
        P(GRP, "tp"),
        P(),
        P(),
        P(GRP, None),
        P(None, GRP_TP),
        P(None, GRP_TP),
        P(GRP_TP, None),
    )
    return jax.shard_map(
        per_device, mesh=split, in_specs=placed, out_specs=P(GRP, "tp"), check_vma=False
    )
```

profile of v0, /device:TPU:8, one launch (start us, length us, event | category | flops | bytes accessed | tf_op | source)
XLA Modules:
  0.0 348.9 jit_solution(12286566533400413660)
XLA Ops:
  6.5 0.0 copy-start
  6.5 1.2 fusion.8
  7.7 0.6 broadcast_in_dim.10
  8.3 5.7 %all-to-all-start = ((f32[8,64,1]{1,2,0:T(1,128)}), f32[8,64,1]{1,2,0:T(1,128)S(1)}, u32[]{:S(2)}, u32[]{:S(2)}) async-start(f32[8,64,1]{1,2,0:T(1,128)} %broadcast_in_dim.10), calls=%async_computation | async-start | bytes 8192 | tf_op jit(solution)/shard_map/all_to_all | solution.py:19
  14.0 0.0 all-gather.2.cloned.1.call-start
  14.0 0.8 slice_bitcast_fusion.1
  14.8 0.1 copy.20
  14.9 0.1 reduce_window_sum.11
  15.0 0.1 copy.21
  15.0 0.8 dynamic_slice.6
  15.8 4.2 %all-to-all-done = f32[8,64,1]{1,2,0:T(1,128)S(1)} async-done(((f32[8,64,1]{1,2,0:T(1,128)}), f32[8,64,1]{1,2,0:T(1,128)S(1)}, u32[]{:S(2)}, u32[]{:S(2)}) %all-to-all-start) | async-done | bytes 2080 | tf_op jit(solution)/shard_map/all_to_all | solution.py:19
  20.1 1.2 convolution_convert_fusion.1
  21.4 1.0 broadcast_in_dim.24
  22.4 1.9 broadcast_in_dim.25
  24.3 1.1 broadcast_in_dim.26
  25.4 4.4 %all_to_all.25 = bf16[16,2,1,18,768]{4,0,3,2,1:T(8,128)(2,1)S(1)} all-to-all(bf16[16,2,1,18,768]{4,0,3,2,1:T(8,128)(2,1)S(1)} %broadcast_in_dim.26), channel_id=1, replica_groups=mesh['grp_0'=4,'grp_1'=4,'grp_2'=2,'tp'=8] {'grp_2'}, dimensions={1} | all-to-all | bytes 1769472 | tf_op jit(solution)/shard_map/all_to_all | solution.py:42
  29.8 0.9 copy.23
  30.7 34.9 %all_to_all.26 = bf16[16,2,1,18,768]{4,1,3,2,0:T(2,128)(2,1)S(1)} all-to-all(bf16[16,2,1,18,768]{4,1,3,2,0:T(2,128)(2,1)S(1)} %copy.23), channel_id=1, replica_groups=mesh['grp_0'=4,'grp_1'=4,'grp_2'=2,'tp'=8] {'grp_0','grp_1'}, dimensions={0} | all-to-all | bytes 1769472 | tf_op jit(solution)/shard_map/all_to_all | solution.py:42
  65.6 1.8 copy.24
  67.4 3.1 reshape_reshape.3
  70.5 0.0 all-gather.2.cloned.1.call-update
  70.6 0.0 reduce-scatter.2.cloned.1.call-start
  70.6 77.7 %all-gather.2.cloned.1.call-done = bf16[32,18,6144]{2,0,1:T(8,128)(2,1)} async-done(((bf16[32,18,768]{2,0,1:T(8,128)(2,1)}), bf16[32,18,6144]{2,0,1:T(8,128)(2,1)}) %all-gather.2.cloned.1.call-update) | async-done | bytes 7077904 | tf_op jit(solution)/shard_map/all_gather | solution.py:53
  148.3 10.7 %copy.25 = bf16[32,18,6144]{2,1,0:T(8,128)(2,1)} copy(bf16[32,18,6144]{2,0,1:T(8,128)(2,1)} %all-gather.2.cloned.1.call-done) | data formatting | bytes 14155776 | tf_op jit(solution)/shard_map/all_gather | solution.py:53
  159.0 9.6 %reshape.146 = bf16[576,6144]{1,0:T(8,128)(2,1)} reshape(bf16[32,18,6144]{2,1,0:T(8,128)(2,1)} %copy.25) | data formatting | bytes 14155776 | tf_op jit(solution)/shard_map/reshape | solution.py:55
  168.7 6.7 %fusion.37 = f32[576,256]{1,0:T(8,128)} fusion(bf16[576,6144]{1,0:T(8,128)(2,1)} %reshape.146, bf16[6144,256]{1,0:T(8,128)(2,1)} %param.11), kind=kOutput, calls=%fused_computation.59 | convolution fusion | flops 1811939328 | bytes 10813440 | tf_op jit(solution)/shard_map/dot_general | solution.py:56
  175.4 0.0 copy-done
  175.4 14.3 %convolution_convert_fusion = bf16[576,6144]{1,0:T(8,128)(2,1)} fusion(bf16[256,6144]{1,0:T(8,128)(2,1)S(1)} %copy-done, bf16[576,6144]{1,0:T(8,128)(2,1)} %reshape.146, bf16[6144,256]{1,0:T(8,128)(2,1)} %param.12, f32[576,256]{1,0:T(8,128)} %fusion.37), kind=kOutput, calls=%fused_computation | convolution fusion | flops 3628302336 | bytes 21037056 | tf_op jit(solution)/shard_map/dot_general | solution.py:59
  189.7 9.5 %reshape.147 = bf16[32,18,6144]{2,1,0:T(8,128)(2,1)} reshape(bf16[576,6144]{1,0:T(8,128)(2,1)} %convolution_convert_fusion) | data formatting | bytes 14155776 | tf_op jit(solution)/shard_map/reshape | solution.py:62
  199.2 0.0 copy-start.1
  199.2 0.0 reduce-scatter.2.cloned.1.call-update
  199.2 0.9 copy-done.1
  200.1 0.9 fusion.23
  201.0 0.1 reshape.154
  201.1 8.7 %all_to_all.27 = f32[8,1,512]{2,1,0:T(1,128)S(1)} all-to-all(f32[8,1,512]{2,1,0:T(1,128)S(1)} %reshape.154), channel_id=1, replica_groups=mesh['grp_0'=4,'grp_1'=4,'grp_2'=2,'tp'=8] {'tp'}, dimensions={0} | all-to-all | bytes 32768 | tf_op jit(solution)/shard_map/all_to_all | solution.py:19
  209.8 93.5 %reduce-scatter.2.cloned.1.call-done = bf16[32,18,768]{2,1,0:T(8,128)(2,1)} async-done(((bf16[32,18,6144]{2,1,0:T(8,128)(2,1)}), bf16[32,18,768]{2,1,0:T(8,128)(2,1)}) %reduce-scatter.2.cloned.1.call-update) | async-done | bytes 884752 | tf_op jit(solution)/shard_map/reduce_scatter | solution.py:64
  303.3 9.3 %all-to-all-start.4 = ((bf16[32,18,768]{2,1,0:T(8,128)(2,1)}), bf16[32,18,768]{2,1,0:T(8,128)(2,1)}, u32[]{:S(2)}, u32[]{:S(2)}) async-start(bf16[32,18,768]{2,1,0:T(8,128)(2,1)} %reduce-scatter.2.cloned.1.call-done), calls=%async_computation.5 | async-start | bytes 2359296 | tf_op jit(solution)/shard_map/all_to_all | solution.py:68
  312.6 0.5 broadcast.113
  313.1 0.7 reduce.1
  313.8 0.1 reshape.155
  314.0 25.7 %all-to-all-done.4 = bf16[32,18,768]{2,1,0:T(8,128)(2,1)} async-done(((bf16[32,18,768]{2,1,0:T(8,128)(2,1)}), bf16[32,18,768]{2,1,0:T(8,128)(2,1)}, u32[]{:S(2)}, u32[]{:S(2)}) %all-to-all-start.4) | async-done | bytes 884768 | tf_op jit(solution)/shard_map/all_to_all | solution.py:68
  339.7 1.5 convert_reduce_fusion
  341.2 0.9 fusion.1
  (11 shorter events, 0.2 us)
Async XLA Ops:
  6.5 168.8 %copy-start = (bf16[256,6144]{1,0:T(8,128)(2,1)S(1)}, bf16[256,6144]{1,0:T(8,128)(2,1)}, u32[]{:S(2)}) copy-start(bf16[256,6144]{1,0:T(8,128)(2,1)} %param.13) | copy-start | bytes 9437188
  8.3 11.8 %all-to-all-start = ((f32[8,64,1]{1,2,0:T(1,128)}), f32[8,64,1]{1,2,0:T(1,128)S(1)}, u32[]{:S(2)}, u32[]{:S(2)}) async-start(f32[8,64,1]{1,2,0:T(1,128)} %broadcast_in_dim.10), calls=%async_computation | async-start | bytes 8192 | tf_op jit(solution)/shard_map/all_to_all | solution.py:19
  14.0 134.3 %all-gather.2.cloned.1.call-start = ((), (), s32[]{:S(2)}) async-start(), calls=%async_computation.6 | async-start | bytes 7962624 | tf_op jit(solution)/shard_map/all_gather | solution.py:53
  70.6 232.8 %reduce-scatter.2.cloned.1.call-start = ((), (), s32[]{:S(2)}) async-start(), calls=%async_computation.7 | async-start | bytes 10616832 | tf_op jit(solution)/shard_map/reduce_scatter | solution.py:64
  199.2 0.9 copy-start.1
  303.3 36.4 %all-to-all-start.4 = ((bf16[32,18,768]{2,1,0:T(8,128)(2,1)}), bf16[32,18,768]{2,1,0:T(8,128)(2,1)}, u32[]{:S(2)}, u32[]{:S(2)}) async-start(bf16[32,18,768]{2,1,0:T(8,128)(2,1)} %reduce-scatter.2.cloned.1.call-done), calls=%async_computation.5 | async-start | bytes 2359296 | tf_op jit(solution)/shard_map/all_to_all | solution.py:68
Sparse Core Ops, SparseCore 0:
  70.7 77.5 all-gather.1
  199.3 103.9 reduce-scatter.1
where the time goes:
time: 355 us; the launch traced here: 349 us
  waiting for transfers between devices  201 us (57%)
  blocking collectives  48 us (14%)
  local copies, waits for them, and re-layouts  43.6 us (12%)
  matrix products  24 us (7%)
  starting transfers between devices  15 us (4%)
  between operations  13.5 us (4%)
    reduce_scatter x1, waiting for transfers between devices, expert_rows(): lax.psum_scatter(partial_out, 'tp', scatter_dimension=2, tiled=True)  93.5 us
    all_gather x1, waiting for transfers between devices, expert_rows(): received = lax.all_gather(received, 'tp', axis=2, tiled=True)  77.7 us
    all_to_all x2, blocking collectives, exchange_in_order(): out = lax.all_to_all(out, axes[k], k, k, tiled=True)  39.3 us
    all_to_all x1, waiting for transfers between devices, expert_rows(): lax.all_to_all(own_share, GRP, split_axis=0, concat_axis=0, tiled=True)  25.7 us
    dot_general x1, matrix products, expert_rows(): jnp.dot(hidden, down_proj, preferred_element_type=jnp.float32)  14.3 us
    all_gather x1, local copies, waits for them, and re-layouts, expert_rows(): received = lax.all_gather(received, 'tp', axis=2, tiled=True)  10.7 us
    reshape x1, local copies, waits for them, and re-layouts, expert_rows(): row_block = received.reshape(source_groups * slot_count, feature_width)  9.63 us
    reshape x1, local copies, waits for them, and re-layouts, expert_rows(): partial_out = partial_out.reshape(source_groups, slot_count, feature_width)  9.49 us
  transfers between devices with their start and end apart: 4, of which 4 were waited for; matrix products, arithmetic and copies ran while one was open for 1% of the time, Pallas kernels for 0%

commit v1 on v0

v1 whole, which is shorter than its diff:
```python
import functools

import jax
import jax.numpy as jnp
import numpy as np
from jax import lax
from jax.experimental import pallas as pl
from jax.experimental.pallas import tpu as pltpu
from jax.sharding import Mesh
from jax.sharding import PartitionSpec as P

AXES = ("zh", "y", "core", "zl", "x")
GRP = ("zh", "y", "core")
TP = ("zl", "x")
CAP = 18
SLOT = 24
BLOCKS = 8
ROWS = BLOCKS * CAP
EPS = 1e-05
F32 = jnp.float32
BF16 = jnp.bfloat16
MESH = pl.DeviceIdType.MESH

RA, RB, RC, RD = (0, 48), (48, 32), (80, 32), (112, 32)


def rows_of(cut):
    return pl.ds(cut[0], cut[1])


def halves(cut):
    half = cut[1] // 2
    return (cut[0], half), (cut[0] + half, half)


def kernel(
    tokens,
    gain,
    router,
    ids,
    pack,
    gate_hbm,
    up_hbm,
    down_hbm,
    out,
    stats_own,
    stats_in,
    logit_own,
    logit_in,
    sent,
    landed,
    G,
    S,
    Q,
    P1,
    final,
    xa_step1,
    xa_step2,
    a_mid,
    a_last,
    c_far,
    c_mid,
    c_step1,
    c_step2,
    leave,
    back,
    gate_w,
    up_w,
    down_w,
    gate_acc,
    up_acc,
    hidden,
    weight_sem,
    send_sem,
    recv_sem,
):
    zh, y, core = lax.axis_index("zh"), lax.axis_index("y"), lax.axis_index("core")
    zl, x = lax.axis_index("zl"), lax.axis_index("x")
    yi = lax.rem(y, 2)
    pair = lax.div(y, 2)
    piece = zl * 4 + x
    width = tokens.shape[1]
    toks = tokens.shape[0]
    xr, xl, xo = lax.rem(x + 1, 4), lax.rem(x + 3, 4), lax.rem(x + 2, 4)
    y_other, z_other = 1 - yi, 1 - zl
    right, left = {"x": xr}, {"x": xl}
    across_y = {"y": pair * 2 + y_other}
    across_z = {"zl": z_other}
    across_core = {"core": 1 - core}

    peers = []
    for dz in range(2):
        for dx in range(4):
            if dz or dx:
                peers.append({"zl": lax.rem(zl + dz, 2), "x": lax.rem(x + dx, 4)})
    homes = []
    for dz in range(4):
        for k in range(2):
            homes.append({"zh": lax.rem(zh + dz, 4), "y": y if k == 0 else 3 - y})
    sources = []
    for dz in range(4):
        for k in range(2):
            sources.append({"zh": lax.rem(zh + 4 - dz, 4), "y": y if k == 0 else 3 - y})

    barrier = pltpu.get_barrier_semaphore()
    greeted = peers + homes[1:] + [across_y, across_core]
    for who in greeted:
        pl.semaphore_signal(barrier, inc=1, device_id=who, device_id_type=MESH)

    loads = [
        pltpu.make_async_copy(src, dst, weight_sem.at[i])
        for i, (src, dst) in enumerate(((gate_hbm, gate_w), (up_hbm, up_w), (down_hbm, down_w)))
    ]
    for load in loads:
        load.start()

    counter = [0]
    started = []

    def send(src, dst, who):
        i = counter[0]
        counter[0] += 1
        copy = pltpu.make_async_remote_copy(
            src_ref=src,
            dst_ref=dst,
            send_sem=send_sem.at[i],
            recv_sem=recv_sem.at[i],
            device_id=who,
            device_id_type=MESH,
        )
        copy.start()
        started.append(copy)
        return copy

    local = tokens[...].astype(F32)
    column = jnp.sum(local * local, axis=-1, keepdims=True)
    stats_own[...] = jnp.transpose(jnp.broadcast_to(column, (toks, 128)))[0:8, :]
    pl.semaphore_wait(barrier, len(greeted))
    stat_copies = [send(stats_own, stats_in.at[i], who) for i, who in enumerate(peers)]

    sub = lax.broadcasted_iota(jnp.int32, (8, toks), 0)
    expert_of = lax.rem(zh + lax.div(sub, 2), 4) * 2 + lax.rem(pair + lax.rem(sub, 2), 2)
    first = ids[0:1, :] == expert_of
    second = ids[1:2, :] == expert_of
    hit = (first | second).astype(F32)
    upper = (
        lax.broadcasted_iota(jnp.int32, (toks, toks), 0)
        <= lax.broadcasted_iota(jnp.int32, (toks, toks), 1)
    ).astype(F32)
    place = jnp.dot(hit.astype(BF16), upper.astype(BF16), preferred_element_type=F32)
    place = jnp.where(hit > 0.5, place - 1.0, -1.0).astype(jnp.int32)
    slot_iota = lax.broadcasted_iota(jnp.int32, (SLOT, toks), 0)

    for copy in stat_copies:
        copy.wait_recv()
    total = stats_own[...]
    for i in range(len(peers)):
        total = total + stats_in[i]
    scale = lax.rsqrt(total / (8 * width) + EPS)
    scale = jnp.transpose(jnp.broadcast_to(scale[0:1, :], (128, toks)))[:, 0:1]
    gain_part = gain[:, pl.ds(pl.multiple_of(piece * width, 128), width)]
    normed = (tokens[...].astype(F32) * scale * gain_part).astype(BF16)

    for b in range(BLOCKS):
        pick = (place[b : b + 1, :] == slot_iota).astype(F32).astype(BF16)
        rows = jnp.dot(pick, normed, preferred_element_type=F32).astype(BF16)
        if b == 0:
            landed[0] = rows
        else:
            sent[b] = rows
    dispatch = [send(sent.at[b], landed.at[b], homes[b]) for b in range(1, BLOCKS)]

    router_part = router[:, pl.ds(pl.multiple_of(piece * width, 128), width)]
    logit_own[...] = lax.dot_general(
        router_part, normed, (((1,), (1,)), ((), ())), preferred_element_type=F32
    )
    logit_copies = [send(logit_own, logit_in.at[i], who) for i, who in enumerate(peers)]

    for copy in dispatch:
        copy.wait_recv()
    G[0, yi, zl, x] = jnp.dot(
        pack[...],
        landed[...].reshape(BLOCKS * SLOT, width),
        preferred_element_type=F32,
    ).astype(BF16)

    ra, rb, rc, rd = rows_of(RA), rows_of(RB), rows_of(RC), rows_of(RD)
    (c0, c1), (d0, d1) = halves(RC), halves(RD)

    def spread(at, who):
        return send(G.at[at], G.at[at], who)

    a1 = spread((0, yi, zl, x, ra), across_y)
    b1 = spread((0, yi, zl, x, rb), across_z)
    c1p = spread((0, yi, zl, x, rc), right)
    c1m = spread((0, yi, zl, x, rc), left)
    d1p = spread((0, yi, zl, x, rd), right)
    d1m = spread((0, yi, zl, x, rd), left)
    a1.wait_recv()
    a2 = spread((0, slice(None), zl, x, ra), across_z)
    b1.wait_recv()
    b2 = spread((0, yi, slice(None), x, rb), across_y)
    c1p.wait_recv()
    c2p = spread((0, yi, zl, xl, rows_of(c0)), right)
    c1m.wait_recv()
    c2m = spread((0, yi, zl, xr, rows_of(c1)), left)
    d1p.wait_recv()
    d2p = spread((0, yi, zl, xl, rows_of(d0)), right)
    d1m.wait_recv()
    d2m = spread((0, yi, zl, xr, rows_of(d1)), left)
    a2.wait_recv()
    a3p = spread((0, slice(None), slice(None), x, ra), right)
    a3m = spread((0, slice(None), slice(None), x, ra), left)
    b2.wait_recv()
    b3p = spread((0, slice(None), slice(None), x, rb), right)
    b3m = spread((0, slice(None), slice(None), x, rb), left)
    c2p.wait_recv()
    c2m.wait_recv()
    c3 = spread((0, yi, zl, slice(None), rc), across_y)
    d2p.wait_recv()
    d2m.wait_recv()
    d3 = spread((0, yi, zl, slice(None), rd), across_z)
    c3.wait_recv()
    c4 = spread((0, slice(None), zl, slice(None), rc), across_z)
    d3.wait_recv()
    d4 = spread((0, yi, slice(None), slice(None), rd), across_y)
    a3p.wait_recv()
    a4p = spread((0, 0, slice(None), xl, ra), right)
    a3m.wait_recv()
    a4m = spread((0, 1, slice(None), xr, ra), left)
    b3p.wait_recv()
    b4p = spread((0, 0, slice(None), xl, rb), right)
    b3m.wait_recv()
    b4m = spread((0, 1, slice(None), xr, rb), left)
    for copy in (a4p, a4m, b4p, b4m, c4, d4):
        copy.wait_recv()

    cores_in = [
        send(G.at[0, :, p // 4, p % 4], G.at[1, :, p // 4, p % 4], across_core) for p in range(8)
    ]
    loads[0].wait()
    loads[1].wait()

    def half_ff(plane, waits):
        gate_acc[...] = jnp.zeros_like(gate_acc)
        up_acc[...] = jnp.zeros_like(up_acc)

        def step(p):
            at = pl.ds(pl.multiple_of(p * width, 128), width)
            block = G[plane, :, lax.div(p, 4), lax.rem(p, 4)].reshape(2 * ROWS, width)
            gate_acc[...] += jnp.dot(block, gate_w[at, :], preferred_element_type=F32)
            up_acc[...] += jnp.dot(block, up_w[at, :], preferred_element_type=F32)

        if waits is not None:
            for copy in waits:
                copy.wait_recv()
        pl.loop(0, 8)(step)
        act = gate_acc[...]
        hidden[plane] = (act / (1.0 + jnp.exp(-act)) * up_acc[...]).astype(BF16)

    half_ff(0, None)
    half_ff(1, cores_in)
    loads[2].wait()

    def partial_out(plane, p):
        at = pl.ds(pl.multiple_of(p * width, 128), width)
        return jnp.dot(hidden[plane], down_w[:, at], preferred_element_type=F32)

    base = counter[0]
    counter[0] += 8

    def core_copy(p):
        return pltpu.make_async_remote_copy(
            src_ref=P1.at[:, lax.div(p, 4), lax.rem(p, 4)],
            dst_ref=Q.at[:, lax.div(p, 4), lax.rem(p, 4)],
            send_sem=send_sem.at[base + p],
            recv_sem=recv_sem.at[base + p],
            device_id=across_core,
            device_id_type=MESH,
        )

    @pl.loop(0, 8)
    def _(p):
        P1[:, lax.div(p, 4), lax.rem(p, 4)] = (
            partial_out(1, p).astype(BF16).reshape(2, ROWS, width)
        )
        core_copy(p).start()

    @pl.loop(0, 8)
    def _(p):
        product = partial_out(0, p)
        core_copy(p).wait_recv()
        theirs = Q[:, lax.div(p, 4), lax.rem(p, 4)].reshape(2 * ROWS, width)
        S[:, lax.div(p, 4), lax.rem(p, 4)] = (
            (product + theirs.astype(F32)).astype(BF16).reshape(2, ROWS, width)
        )

    def add(dst, src):
        S[dst] = (S[dst].astype(F32) + src.astype(F32)).astype(BF16)

    def a_ops(cut, i):
        n = cut[1]
        r = rows_of(cut)
        at = pl.ds(cut[0], n)
        step1p = send(S.at[0, :, xo, r], xa_step1.at[0, :, at], right)
        step1m = send(S.at[1, :, xo, r], xa_step1.at[1, :, at], left)
        return r, at, step1p, step1m

    ar, aat, a1p, a1m = a_ops(RA, 0)
    br, bat, b1p, b1m = a_ops(RB, 1)
    cc1 = send(S.at[:, z_other, :, rc], c_far.at[0], across_z)
    dd1 = send(S.at[y_other, :, :, rd], c_far.at[1], across_y)

    def x_second(r, at, p1, m1):
        p1.wait_recv()
        for k in range(2):
            add((0, k, xr, r), xa_step1[0, k, at])
        p2 = send(S.at[:, :, xr, r], xa_step2.at[0, :, :, at], right)
        m1.wait_recv()
        for k in range(2):
            add((1, k, xl, r), xa_step1[1, k, at])
        m2 = send(S.at[:, :, xl, r], xa_step2.at[1, :, :, at], left)
        return p2, m2

    a2p, a2m = x_second(ar, aat, a1p, a1m)
    b2p, b2m = x_second(br, bat, b1p, b1m)

    cc1.wait_recv()
    for j in range(2):
        for k in range(4):
            add((j, zl, k, rc), c_far[0, j, k])
    cc2 = send(S.at[y_other, zl, :, rc], c_mid.at[0], across_y)
    dd1.wait_recv()
    for j in range(2):
        for k in range(4):
            add((yi, j, k, rd), c_far[1, j, k])
    dd2 = send(S.at[yi, z_other, :, rd], c_mid.at[1], across_z)

    def x_done(r, at, p2, m2):
        p2.wait_recv()
        m2.wait_recv()
        for j in range(2):
            for k in range(2):
                S[j, k, x, r] = (
                    S[j, k, x, r].astype(F32)
                    + xa_step2[0, j, k, at].astype(F32)
                    + xa_step2[1, j, k, at].astype(F32)
                ).astype(BF16)

    x_done(ar, aat, a2p, a2m)
    a3 = send(S.at[:, z_other, x, ar], a_mid.at[:, aat], across_z)
    x_done(br, bat, b2p, b2m)
    b3 = send(S.at[y_other, :, x, br], a_mid.at[:, bat], across_y)

    def last_x_first(cut, i, mid_copy):
        n = cut[1]
        r = rows_of(cut)
        mid_copy.wait_recv()
        for k in range(4):
            add((yi, zl, k, r), c_mid[i, k])
        lo, hi = halves(cut)
        p1 = send(S.at[yi, zl, xo, rows_of(lo)], c_step1.at[i, 0], right)
        m1 = send(S.at[yi, zl, xo, rows_of(hi)], c_step1.at[i, 1], left)
        return r, lo, hi, p1, m1

    cx = last_x_first(RC, 0, cc2)
    dx = last_x_first(RD, 1, dd2)

    def last_x_second(i, r, lo, hi, p1, m1):
        p1.wait_recv()
        add((yi, zl, xr, rows_of(lo)), c_step1[i, 0])
        p2 = send(S.at[yi, zl, xr, r], c_step2.at[i, 0], right)
        m1.wait_recv()
        add((yi, zl, xl, rows_of(hi)), c_step1[i, 1])
        m2 = send(S.at[yi, zl, xl, r], c_step2.at[i, 1], left)
        return p2, m2

    a3.wait_recv()
    for k in range(2):
        add((k, zl, x, ar), a_mid[k, aat])
    a4 = send(S.at[y_other, zl, x, ar], a_last.at[aat], across_y)
    b3.wait_recv()
    for k in range(2):
        add((yi, k, x, br), a_mid[k, bat])
    b4 = send(S.at[yi, z_other, x, br], a_last.at[bat], across_z)

    cx2 = last_x_second(0, *cx)
    dx2 = last_x_second(1, *dx)

    a4.wait_recv()
    final[ar] = (S[yi, zl, x, ar].astype(F32) + a_last[aat].astype(F32)).astype(BF16)
    b4.wait_recv()
    final[br] = (S[yi, zl, x, br].astype(F32) + a_last[bat].astype(F32)).astype(BF16)
    for i, (r, (p2, m2)) in enumerate(((rc, cx2), (rd, dx2))):
        p2.wait_recv()
        m2.wait_recv()
        final[r] = (
            S[yi, zl, x, r].astype(F32) + c_step2[i, 0].astype(F32) + c_step2[i, 1].astype(F32)
        ).astype(BF16)

    opened = lax.dot_general(
        pack[...], final[...], (((0,), (0,)), ((), ())), preferred_element_type=F32
    ).astype(BF16)
    for b in range(BLOCKS):
        block = opened[b * SLOT : (b + 1) * SLOT]
        if b == 0:
            back[0] = block
        else:
            leave[b] = block
    returns = [send(leave.at[b], back.at[b], sources[b]) for b in range(1, BLOCKS)]

    for copy in logit_copies:
        copy.wait_recv()
    logits = logit_own[...]
    for i in range(len(peers)):
        logits = logits + logit_in[i]
    expert_row = sub
    l0 = jnp.sum(jnp.where(ids[0:1, :] == expert_row, logits, 0.0), axis=0, keepdims=True)
    l1 = jnp.sum(jnp.where(ids[1:2, :] == expert_row, logits, 0.0), axis=0, keepdims=True)
    g0 = 1.0 / (1.0 + jnp.exp(l1 - l0))
    g1 = 1.0 / (1.0 + jnp.exp(l0 - l1))
    share = jnp.where(first, g0, 0.0) + jnp.where(second, g1, 0.0)
    weights = jnp.concatenate(
        [
            jnp.where(place[b : b + 1, :] == slot_iota, share[b : b + 1, :], 0.0)
            for b in range(BLOCKS)
        ],
        axis=0,
    )
    high = weights.astype(BF16)
    low = (weights - high.astype(F32)).astype(BF16)
    for copy in returns:
        copy.wait_recv()
    rows = back[...].reshape(BLOCKS * SLOT, width)
    dims = (((0,), (0,)), ((), ()))
    out[...] = (
        lax.dot_general(high, rows, dims, preferred_element_type=F32)
        + lax.dot_general(low, rows, dims, preferred_element_type=F32)
    ).astype(BF16)

    for copy in started:
        copy.wait_send()

    @pl.loop(0, 8)
    def _(p):
        core_copy(p).wait_send()


def per_device(tokens, norm_gain, router_weight, expert_ids, gate_proj, up_proj, down_proj):
    toks, width = tokens.shape
    hid = gate_proj.shape[1]
    pack = np.zeros((ROWS, BLOCKS * SLOT), np.float32)
    for r in range(ROWS):
        pack[r, r // CAP * SLOT + r % CAP] = 1.0
    vmem = pl.BlockSpec(memory_space=pltpu.VMEM)
    anywhere = pl.BlockSpec(memory_space=pl.ANY)
    n_ab = RA[1] + RB[1]
    n_c = RC[1]
    big = (2, 2, 4, ROWS, width)
    messages = 120
    return pl.pallas_call(
        kernel,
        out_shape=jax.ShapeDtypeStruct((toks, width), BF16),
        in_specs=[vmem] * 5 + [anywhere] * 3,
        out_specs=vmem,
        scratch_shapes=[
            pltpu.VMEM((8, toks), F32),
            pltpu.VMEM((7, 8, toks), F32),
            pltpu.VMEM((8, toks), F32),
            pltpu.VMEM((7, 8, toks), F32),
            pltpu.VMEM((BLOCKS, SLOT, width), BF16),
            pltpu.VMEM((BLOCKS, SLOT, width), BF16),
            pltpu.VMEM((2,) + big, BF16),
            pltpu.VMEM(big, BF16),
            pltpu.VMEM(big, BF16),
            pltpu.VMEM(big, BF16),
            pltpu.VMEM((ROWS, width), BF16),
            pltpu.VMEM((2, 2, n_ab, width), BF16),
            pltpu.VMEM((2, 2, 2, n_ab, width), BF16),
            pltpu.VMEM((2, n_ab, width), BF16),
            pltpu.VMEM((n_ab, width), BF16),
            pltpu.VMEM((2, 2, 4, n_c, width), BF16),
            pltpu.VMEM((2, 4, n_c, width), BF16),
            pltpu.VMEM((2, 2, n_c // 2, width), BF16),
            pltpu.VMEM((2, 2, n_c, width), BF16),
            pltpu.VMEM((BLOCKS, SLOT, width), BF16),
            pltpu.VMEM((BLOCKS, SLOT, width), BF16),
            pltpu.VMEM(gate_proj.shape, BF16),
            pltpu.VMEM(up_proj.shape, BF16),
            pltpu.VMEM(down_proj.shape, BF16),
            pltpu.VMEM((2 * ROWS, hid), F32),
            pltpu.VMEM((2 * ROWS, hid), F32),
            pltpu.VMEM((2, 2 * ROWS, hid), BF16),
            pltpu.SemaphoreType.DMA((3,)),
            pltpu.SemaphoreType.DMA((messages,)),
            pltpu.SemaphoreType.DMA((messages,)),
        ],
        compiler_params=pltpu.CompilerParams(
            collective_id=0, has_side_effects=True, vmem_limit_bytes=63 * 1024 * 1024
        ),
        name="routed_block",
    )(
        tokens,
        norm_gain.reshape(1, -1),
        router_weight.T,
        expert_ids.T,
        jnp.asarray(pack, BF16),
        gate_proj,
        up_proj,
        down_proj,
    )


def solution(mesh):
    split = Mesh(mesh.devices.reshape(4, 4, 2, 2, 4), AXES)
    every = GRP + TP
    placed = (
        P(GRP, TP),
        P(),
        P(),
        P(GRP, None),
        P(None, every),
        P(None, every),
        P(every, None),
    )
    return jax.shard_map(
        per_device, mesh=split, in_specs=placed, out_specs=P(GRP, TP), check_vma=False
    )
```

time: 355 us -> 102 us (0.29); the launches traced: 349 us -> 102 us
  waiting for transfers between devices: 201 us -> 0 us
  Pallas kernels: 0 us -> 100 us
  blocking collectives: 48 us -> 0 us
  local copies, waits for them, and re-layouts: 43.6 us -> 1.54 us
  matrix products: 24 us -> 0 us
  starting transfers between devices: 15 us -> 0 us
  between operations: 13.5 us -> 0.01 us
    pallas_call x0 -> x1, Pallas kernels: none -> 100 us  [per_device(): pl.pallas_call(kernel, out_shape=jax.ShapeDtypeStruct((toks, width), BF16...]
    reduce_scatter x1 -> x0, waiting for transfers between devices: 93.5 us -> none  [expert_rows(): lax.psum_scatter(partial_out, 'tp', scatter_dimension=2, tiled=True)]
    all_gather x1 -> x0, waiting for transfers between devices: 77.7 us -> none  [expert_rows(): received = lax.all_gather(received, 'tp', axis=2, tiled=True)]
    all_to_all x3 -> x0, blocking collectives: 48 us -> none  [the longest x2 39.3 us: exchange_in_order(): out = lax.all_to_all(out, axes[k], k, k, tiled=True)]
    all_to_all x2 -> x0, waiting for transfers between devices: 30 us -> none  [the longest x1 25.7 us: expert_rows(): lax.all_to_all(own_share, GRP, split_axis=0, concat_axis=0, tiled=True)]
    dot_general x5 -> x0, matrix products: 24 us -> none  [the longest x1 14.3 us: expert_rows(): jnp.dot(hidden, down_proj, preferred_element_type=jnp.float32)]
    reshape x2 -> x0, local copies, waits for them, and re-layouts: 19.1 us -> none  [the longest x1 9.63 us: expert_rows(): row_block = received.reshape(source_groups * slot_count, feature_width)]
    all_to_all x2 -> x0, starting transfers between devices: 15 us -> none  [the longest x1 9.31 us: expert_rows(): lax.all_to_all(own_share, GRP, split_axis=0, concat_axis=0, tiled=True)]
  transfers between devices with their start and end apart: 4 -> 0, of which waited for: 4 -> 0; matrix products, arithmetic and copies ran while one was open for 1% -> 0% of each run, Pallas kernels for 0% -> 0%
where the time goes in v1:
time: 102 us
  Pallas kernels  100 us (98%)
  local copies, waits for them, and re-layouts  1.54 us (2%)
    pallas_call x1, Pallas kernels, per_device(): pl.pallas_call(kernel, out_shape=jax.ShapeDtypeStruct((toks, width), BF16...  100 us

profile of v1, /device:TPU:8, one launch (start us, length us, event | category | flops | bytes accessed | tf_op | source)
XLA Modules:
  0.0 101.7 jit_solution(16065441149262921221)
XLA Ops:
  0.0 100.1 %routed_block.1 = bf16[64,768]{1,0:T(8,128)(2,1)} custom-call(bf16[64,768]{1,0:T(8,128)(2,1)} %tokens.1, f32[1,6144]{1,0:T(1,128)} %bitcast.4, bf16[8,6144]{1,0:T(8,128)(2,1)} %bitcast.3, s32[2,64]{1,0:T(2,128)} %bitcast.5, bf16[144,192]{1,0:T(8,128)(2,1)} %constant.2.clone.pack, bf16[6144,256]{1,0:T(8,128)(2,1)} %gate_hbm.1, bf16[6144,256]{1,0:T(8,128)(2,1)} %up_hbm.1, ...), custom_call_target="tpu_custom_call" | custom-call | tf_op jit(solution)/shard_map/routed_block/pallas_call | solution.py:461
  100.1 1.5 %copy.10 = bf16[64,768]{1,0:T(8,128)(2,1)} copy(bf16[64,768]{1,0:T(8,128)(2,1)} %routed_block.1) | data formatting | bytes 196608
